TPU v7x, 256 devices: a whole 4x4x8 slice. The times are simulated.
256 devices in a mesh: tm: 16 (over x, y), paths: 16 (over z, core).
Axes of the slice: x: 4, y: 4, z: 8, core: 2. Of those that a mesh axis runs over, the one named last changes fastest.
Arguments:
- returns: bfloat16 [512, 8192, 256], P('tm', 'paths'), may hold values from -0.15917969 to 0.15917969
- weights: bfloat16 [256, 64], P('paths'), may hold values from -0.375 to 0.375
Outputs:
- drawdown: float32 [64, 8192], P('tm', 'paths')
All inputs are finite; a program needn't handle non-finite values.
Results may differ from a plain program's by a relative error of at most 0.0003.
Values may be sent and summed in bfloat16 or wider, within the bound.
A program may use at most 64 MiB of HBM per device.

v0:
```python
import jax
import jax.numpy as jnp
from jax import lax
from jax.sharding import PartitionSpec as P

very_large = 1e30


def in_order(pieces, dim):
    lengths = list(pieces.shape[1:])
    lengths[dim] *= pieces.shape[0]
    return jnp.moveaxis(pieces, 0, dim).reshape(lengths)


def from_everyone(array, axis):
    size = lax.axis_size(axis)
    return lax.all_to_all(
        jnp.broadcast_to(array[None], (size, *array.shape)), axis, 0, 0, tiled=True
    )


def gathered_copies(array, axis, dim):
    return in_order(from_everyone(array, axis), dim)


def combined_pairwise(pieces, combine):
    while len(jax.tree.leaves(pieces)[0]) > 1:
        pieces = jax.vmap(combine)(
            *(jax.tree.map(lambda part: part[side::2], pieces) for side in (0, 1))
        )
    return jax.tree.map(lambda part: part[0], pieces)


def carried_in(array, axis, combine, identity):
    size, position = (lax.axis_size(axis), lax.axis_index(axis))
    passed = jnp.arange(size) < position

    def kept(part, zero, own):
        part = jnp.where(
            passed.reshape(-1, *(1 for _ in own.shape)), part, jnp.asarray(zero, own.dtype)
        )
        return part

    pieces = jax.tree.map(lambda part: from_everyone(part, axis), array)
    return combined_pairwise(jax.tree.map(kept, pieces, identity, array), combine)


def join_two(earlier, later):
    return (earlier[0] + later[0], jnp.maximum(earlier[1], earlier[0] + later[1]))


def shards(returns, weights):
    all_weights = gathered_copies(weights, "paths", 0)
    profit = jnp.einsum("tpa,aq->tqp", returns, all_weights, preferred_element_type=jnp.float32)
    steps_here = profit.shape[0]
    row_ids = lax.broadcasted_iota(jnp.int32, (steps_here, steps_here), 0)
    col_ids = lax.broadcasted_iota(jnp.int32, (steps_here, steps_here), 1)
    lower = (row_ids >= col_ids).astype(jnp.float32)
    flat = profit.reshape(steps_here, -1)
    values = jnp.dot(
        lower, flat, precision=lax.Precision.HIGHEST, preferred_element_type=jnp.float32
    ).reshape(profit.shape)
    peaks = jnp.maximum(lax.cummax(values, axis=0), 0.0)
    offset = values[-1]
    highest = peaks[-1]
    segments = lax.axis_size("tm")
    block_width = offset.shape[0] // segments
    zeros = jnp.zeros_like(offset)
    prior_offset, prior_peak = carried_in(
        (offset, highest), "tm", join_two, (zeros, zeros - very_large)
    )
    running = jnp.maximum(prior_peak[None], prior_offset[None] + peaks)
    falls = jnp.max(running - (prior_offset[None] + values), axis=0)
    blocks = falls.reshape(segments, block_width, falls.shape[1])
    received = lax.all_to_all(blocks, "tm", split_axis=0, concat_axis=0, tiled=True)
    return jnp.max(received, axis=0)


def solution(mesh):
    in_specs = (P("tm", "paths", None), P("paths", None))
    out_specs = P("tm", "paths")
    return jax.shard_map(shards, mesh=mesh, in_specs=in_specs, out_specs=out_specs, check_vma=False)
```

profile of v0, /device:TPU:1, one launch (start us, length us, event | category | flops | bytes accessed | tf_op | source)
XLA Modules:
  0.0 120.7 jit_solution(6636606138366388231)
XLA Ops:
  0.0 0.7 broadcast_in_dim.40
  0.7 0.1 reshape.44
  0.8 17.2 %all_to_all.20 = bf16[16,2,512]{2,1,0:T(2,128)(2,1)S(1)} all-to-all(bf16[16,2,512]{2,1,0:T(2,128)(2,1)S(1)} %reshape.44), channel_id=1, replica_groups=mesh['tm'=16,'paths'=16] {'paths'}, dimensions={0} | all-to-all | bytes 65536 | tf_op jit(solution)/shard_map/all_to_all | solution.py:17
  18.0 0.1 reshape.45
  18.1 6.0 %fusion.4 = f32[64,32,512]{2,0,1:T(8,128)S(1)} fusion(bf16[256,64,1]{1,0,2:T(8,128)(2,1)S(1)} %bitcast.30, bf16[32,512,256]{2,1,0:T(8,128)(2,1)} %param.2), kind=kOutput, calls=%fused_computation.20 | convolution fusion | flops 536870912 | bytes 12615680 | tf_op jit(solution)/shard_map/tpa,aq->tqp/dot_general | solution.py:54
  24.1 2.4 %copy.11 = f32[4,8,64,512]{3,1,2,0:T(8,128)S(1)} copy(f32[4,8,64,512]{3,2,1,0:T(8,128)S(1)} %bitcast.24) | data formatting | bytes 8388608
  26.6 2.3 %fusion.3 = f32[32,32768]{1,0:T(8,128)S(1)} fusion(f32[32,32768]{1,0:T(8,128)S(1)} %bitcast.26), kind=kOutput, calls=%fused_computation.18 | convolution fusion | flops 402654208 | bytes 8388608 | tf_op jit(solution)/shard_map/dot_general | solution.py:60
  28.8 0.0 copy-start
  28.8 1.9 %copy-done = f32[32,32768]{1,0:T(8,128)} copy-done((f32[32,32768]{1,0:T(8,128)}, f32[32,32768]{1,0:T(8,128)S(1)}, u32[]{:S(2)}) %copy-start) | copy-done | bytes 4194328
  30.8 0.4 slice_reduce_fusion
  31.2 1.6 %broadcast_in_dim.45 = f32[16,64,512]{2,1,0:T(8,128)} broadcast(f32[64,512]{1,0:T(8,128)S(1)} %broadcast_in_dim.44), dimensions={1,2} | broadcast | bytes 2228224 | tf_op jit(solution)/shard_map/broadcast_in_dim | solution.py:18
  32.8 6.8 %all-to-all-start.2 = ((f32[16,64,512]{2,1,0:T(8,128)}), f32[16,64,512]{2,1,0:T(8,128)S(1)}, u32[]{:S(2)}, u32[]{:S(2)}) async-start(f32[16,64,512]{2,1,0:T(8,128)} %broadcast_in_dim.45), calls=%async_computation.2 | async-start | bytes 4194304 | tf_op jit(solution)/shard_map/all_to_all | solution.py:17
  39.6 4.6 %copy.12 = f32[4,8,64,512]{3,2,1,0:T(8,128)S(1)} copy(f32[4,8,64,512]{3,1,2,0:T(8,128)} %bitcast.22) | data formatting | bytes 8388608
  44.2 20.9 %broadcast_maximum_fusion = f32[32,64,512]{2,1,0:T(8,128)S(1)} fusion(f32[32,64,512]{2,1,0:T(8,128)S(1)} %bitcast.27), kind=kOutput, calls=%fused_computation.1 | output fusion | flops 33554432 | bytes 8388608 | tf_op jit(solution)/shard_map/shards/reduce_window_max | solution.py:63
  65.1 0.0 copy-start.2
  65.1 2.0 %copy-done.2 = f32[32,64,512]{2,1,0:T(8,128)} copy-done((f32[32,64,512]{2,1,0:T(8,128)}, f32[32,64,512]{2,1,0:T(8,128)S(1)}, u32[]{:S(2)}) %copy-start.2) | copy-done | bytes 4194328
  67.1 1.7 %all-to-all-done.2 = f32[16,64,512]{2,1,0:T(8,128)S(1)} async-done(((f32[16,64,512]{2,1,0:T(8,128)}), f32[16,64,512]{2,1,0:T(8,128)S(1)}, u32[]{:S(2)}, u32[]{:S(2)}) %all-to-all-start.2) | async-done | bytes 2097184 | tf_op jit(solution)/shard_map/all_to_all | solution.py:17
  68.8 1.6 %broadcast_in_dim.42 = f32[16,64,512]{2,1,0:T(8,128)} broadcast(f32[64,512]{1,0:T(8,128)S(1)} %slice_bitcast_fusion), dimensions={1,2} | broadcast | bytes 2228224 | tf_op jit(solution)/shard_map/broadcast_in_dim | solution.py:18
  70.3 5.1 %all-to-all-start.1 = ((f32[16,64,512]{2,1,0:T(8,128)}), f32[16,64,512]{2,1,0:T(8,128)}, u32[]{:S(2)}, u32[]{:S(2)}) async-start(f32[16,64,512]{2,1,0:T(8,128)} %broadcast_in_dim.42), calls=%async_computation.1 | async-start | bytes 4194304 | tf_op jit(solution)/shard_map/all_to_all | solution.py:17
  75.4 6.6 %copy.15 = f32[4,8,64,512]{3,1,2,0:T(8,128)} copy(f32[4,8,64,512]{3,2,1,0:T(8,128)} %bitcast.23) | data formatting | bytes 8388608
  82.0 19.3 %all-to-all-done.1 = f32[16,64,512]{2,1,0:T(8,128)} async-done(((f32[16,64,512]{2,1,0:T(8,128)}), f32[16,64,512]{2,1,0:T(8,128)}, u32[]{:S(2)}, u32[]{:S(2)}) %all-to-all-start.1) | async-done | bytes 2097184 | tf_op jit(solution)/shard_map/all_to_all | solution.py:17
  101.3 2.4 %broadcast_select_fusion.1 = (f32[16,64,512]{2,1,0:T(8,128)S(1)}, f32[16,64,512]{2,1,0:T(8,128)S(1)}) fusion(f32[16,64,512]{2,1,0:T(8,128)} %all-to-all-done.1, pred[16]{0:T(512)(128)(4,1)S(1)} %iota_compare_fusion.2, f32[16,64,512]{2,1,0:T(8,128)S(1)} %all-to-all-done.2), kind=kLoop, calls=%fused_computation.5 | loop fusion | flops 1048576 | bytes 8388624 | tf_op jit(solution)/shard_map/jit(_where)/select_n | solution.py:39
  103.7 0.0 copy-start.3
  103.7 0.5 add_maximum_fusion
  104.2 0.0 copy-start.1
  104.2 0.2 add_maximum_fusion.1
  104.5 0.1 add_maximum_fusion.2
  104.7 1.2 copy-done.3
  105.9 1.4 %copy-done.1 = f32[32,32768]{1,0:T(8,128)S(1)} copy-done((f32[32,32768]{1,0:T(8,128)S(1)}, f32[32,32768]{1,0:T(8,128)}, u32[]{:S(2)}) %copy-start.1) | copy-done | bytes 4194328
  107.3 0.9 subtract_reduce_fusion
  108.3 11.8 %all_to_all.21 = f32[16,4,512]{2,1,0:T(4,128)S(1)} all-to-all(f32[16,4,512]{2,1,0:T(4,128)S(1)} %reshape.35), channel_id=1, replica_groups=mesh['tm'=16,'paths'=16] {'tm'}, dimensions={0} | all-to-all | bytes 262144 | tf_op jit(solution)/shard_map/all_to_all | solution.py:75
  120.0 0.6 reduce_max.19
  (7 shorter events, 0.2 us)
Async XLA Ops:
  28.8 1.9 %copy-start = (f32[32,32768]{1,0:T(8,128)}, f32[32,32768]{1,0:T(8,128)S(1)}, u32[]{:S(2)}) copy-start(f32[32,32768]{1,0:T(8,128)S(1)} %fusion.3) | copy-start | bytes 12582916
  32.8 36.0 %all-to-all-start.2 = ((f32[16,64,512]{2,1,0:T(8,128)}), f32[16,64,512]{2,1,0:T(8,128)S(1)}, u32[]{:S(2)}, u32[]{:S(2)}) async-start(f32[16,64,512]{2,1,0:T(8,128)} %broadcast_in_dim.45), calls=%async_computation.2 | async-start | bytes 4194304 | tf_op jit(solution)/shard_map/all_to_all | solution.py:17
  65.1 2.0 %copy-start.2 = (f32[32,64,512]{2,1,0:T(8,128)}, f32[32,64,512]{2,1,0:T(8,128)S(1)}, u32[]{:S(2)}) copy-start(f32[32,64,512]{2,1,0:T(8,128)S(1)} %broadcast_maximum_fusion) | copy-start | bytes 12582916
  70.3 30.9 %all-to-all-start.1 = ((f32[16,64,512]{2,1,0:T(8,128)}), f32[16,64,512]{2,1,0:T(8,128)}, u32[]{:S(2)}, u32[]{:S(2)}) async-start(f32[16,64,512]{2,1,0:T(8,128)} %broadcast_in_dim.42), calls=%async_computation.1 | async-start | bytes 4194304 | tf_op jit(solution)/shard_map/all_to_all | solution.py:17
  103.7 2.2 %copy-start.3 = (f32[4,8,64,512]{3,1,2,0:T(8,128)S(1)}, f32[4,8,64,512]{3,1,2,0:T(8,128)}, u32[]{:S(2)}) copy-start(f32[4,8,64,512]{3,1,2,0:T(8,128)} %copy.15) | copy-start | bytes 12582916
  104.2 3.0 %copy-start.1 = (f32[32,32768]{1,0:T(8,128)S(1)}, f32[32,32768]{1,0:T(8,128)}, u32[]{:S(2)}) copy-start(f32[32,32768]{1,0:T(8,128)} %copy-done) | copy-start | bytes 12582916
where the time goes:
time: 123 us; the launch traced here: 121 us
  blocking collectives  28.9 us (23%)
  other arithmetic  25.8 us (21%)
  local copies, waits for them, and re-layouts  24.7 us (20%)
  waiting for transfers between devices  20.9 us (17%)
  starting transfers between devices  11.8 us (10%)
  matrix products  8.31 us (7%)
    all_to_all x2, waiting for transfers between devices, from_everyone(): lax.all_to_all(jnp.broadcast_to(array[None], (size, *array.shape)), axis,...  20.9 us
    another operation x1, other arithmetic, shards(): peaks = jnp.maximum(lax.cummax(values, axis=0), 0.0)  20.9 us
    unnamed x15, local copies, waits for them, and re-layouts  20.4 us
    all_to_all x1, blocking collectives, from_everyone(): lax.all_to_all(jnp.broadcast_to(array[None], (size, *array.shape)), axis,...  17.2 us
    all_to_all x2, starting transfers between devices, from_everyone(): lax.all_to_all(jnp.broadcast_to(array[None], (size, *array.shape)), axis,...  11.8 us
    all_to_all x1, blocking collectives, shards(): lax.all_to_all(blocks, 'tm', split_axis=0, concat_axis=0, tiled=True)  11.8 us
    dot_general x1, matrix products, shards(): jnp.einsum('tpa,aq->tqp', returns, all_weights, preferred_element_type=jn...  6.03 us
    broadcast_in_dim x5, local copies, waits for them, and re-layouts, from_everyone(): jnp.broadcast_to(array[None], (size, *array.shape))  3.95 us
  transfers between devices with their start and end apart: 2, of which 2 were waited for; matrix products, arithmetic and copies ran while one was open for 27% of the time, Pallas kernels for 0%

commit v1 on v0

v1 whole, which is shorter than its diff:
```python
import jax
import jax.numpy as jnp
from jax import lax
from jax.experimental import pallas as pl
from jax.experimental.pallas import tpu as pltpu
from jax.sharding import PartitionSpec as P

MESH = pl.DeviceIdType.MESH
LANES = 128
SUB = 8


def kernel(n_tm, n_paths, ret_ref, w_ref, out_ref,
           x, w_in, w_all, y, outbox, inbox,
           x_sem, w_in_sem, w_send_sem, w_recv_sem, send_sem, recv_sem):
    tm = lax.axis_index("tm")
    paths = lax.axis_index("paths")
    steps, n_local, assets = ret_ref.shape
    rows, port = w_ref.shape
    chunks = n_local // LANES
    half = steps // 2
    held = port // n_tm

    barrier = pltpu.get_barrier_semaphore()
    for d in range(1, n_paths):
        pl.semaphore_signal(barrier, inc=1, device_id=(tm, lax.rem(paths + d, n_paths)), device_id_type=MESH)
    for d in range(1, n_tm):
        pl.semaphore_signal(barrier, inc=1, device_id=(lax.rem(tm + d, n_tm), paths), device_id_type=MESH)
    w_load = pltpu.make_async_copy(w_ref, w_in, w_in_sem)
    w_load.start()
    loads = []
    for c in range(chunks):
        load = pltpu.make_async_copy(ret_ref.at[:, pl.ds(c * LANES, LANES), :], x.at[c], x_sem.at[c])
        load.start()
        loads.append(load)

    w_load.wait()
    source = lax.broadcasted_iota(jnp.int32, (port, LANES), 0)
    lane = lax.broadcasted_iota(jnp.int32, (port, LANES), 1)
    spread = jnp.where(source == (lane // SUB) * held + lane % held, 1.0, 0.0).astype(jnp.bfloat16)
    own_rows = pl.ds(pl.multiple_of(paths * rows, rows), rows)
    w_all[own_rows, :] = jnp.dot(w_in[...], spread, preferred_element_type=jnp.float32).astype(jnp.bfloat16)

    pl.semaphore_wait(barrier, n_paths - 1 + n_tm - 1)

    w_sends = []
    order = sorted(range(1, n_paths), key=lambda d: -min(d, n_paths - d))
    for d in order:
        copy = pltpu.make_async_remote_copy(
            src_ref=w_all.at[own_rows, :], dst_ref=w_all.at[own_rows, :],
            send_sem=w_send_sem.at[d], recv_sem=w_recv_sem.at[d],
            device_id=(tm, lax.rem(paths + d, n_paths)), device_id_type=MESH)
        copy.start()
        w_sends.append(copy)
    for copy in reversed(w_sends):
        copy.wait_recv()

    lane_w = lax.broadcasted_iota(jnp.int32, (assets, LANES), 1)
    first = (lane_w % SUB) < held
    w_all_now = w_all[...].astype(jnp.float32)
    w_a = jnp.where(first, w_all_now, 0.0).astype(jnp.bfloat16)
    w_b = jnp.where(first, 0.0, w_all_now).astype(jnp.bfloat16)

    second = (lax.broadcasted_iota(jnp.int32, (LANES, LANES), 1) % SUB) >= held
    tm_order = list(range(1, n_tm))
    sends = []
    for c in range(chunks):
        loads[c].wait()
        x_a = x[c, 0:half].reshape(half * LANES, assets)
        x_b = x[c, half:steps].reshape(half * LANES, assets)
        y[...] = (jnp.dot(x_a, w_a, preferred_element_type=jnp.float32)
                  + jnp.dot(x_b, w_b, preferred_element_type=jnp.float32))
        total, high, low, deep = [], [], [], []
        for r in range(0, LANES, 32):
            v = y[pl.ds(r, 32), :]
            hi = jnp.maximum(v, 0.0)
            lo = jnp.minimum(v, 0.0)
            dd = hi - v
            for t in range(1, half):
                v = v + y[pl.ds(t * LANES + r, 32), :]
                hi = jnp.maximum(hi, v)
                lo = jnp.minimum(lo, v)
                dd = jnp.maximum(dd, hi - v)
            total.append(v)
            high.append(hi)
            low.append(lo)
            deep.append(dd)
        total, high, low, deep = (jnp.concatenate(part, axis=0) for part in (total, high, low, deep))
        t0, h0, l0, d0 = (pltpu.roll(part, held, 1) for part in (total, high, low, deep))
        m_total = t0 + total
        m_high = jnp.maximum(h0, t0 + high)
        m_low = jnp.minimum(l0, t0 + low)
        m_deep = jnp.maximum(jnp.maximum(d0, deep), h0 - (t0 + low))
        th = jnp.where(second, m_high, pltpu.roll(m_total, LANES - held, 1))
        ld = jnp.where(second, m_deep, pltpu.roll(m_low, LANES - held, 1))
        outbox[c, :, 0] = th.T.reshape(n_tm, SUB, LANES)
        outbox[c, :, 1] = ld.T.reshape(n_tm, SUB, LANES)
        for d in tm_order:
            to = lax.rem(tm + d, n_tm)
            copy = pltpu.make_async_remote_copy(
                src_ref=outbox.at[c, to], dst_ref=inbox.at[c, tm],
                send_sem=send_sem.at[c, d], recv_sem=recv_sem.at[c, d],
                device_id=(to, paths), device_id_type=MESH)
            copy.start()
            sends.append(copy)
        inbox[c, pl.ds(tm, 1)] = outbox[c, pl.ds(tm, 1)]

    for c in range(chunks):
        for copy in sends[c * len(tm_order):(c + 1) * len(tm_order)]:
            copy.wait_recv()
        offset = jnp.zeros((SUB, LANES), jnp.float32)
        peak = jnp.zeros((SUB, LANES), jnp.float32)
        fall = jnp.zeros((SUB, LANES), jnp.float32)
        for s in range(n_tm):
            th = inbox[c, s, 0]
            ld = inbox[c, s, 1]
            fall = jnp.maximum(fall, jnp.maximum(pltpu.roll(ld, held, 0), peak - (offset + ld)))
            peak = jnp.maximum(peak, offset + pltpu.roll(th, held, 0))
            offset = offset + th
        out_ref[:, pl.ds(c * LANES, LANES)] = fall[:held]

    for copy in w_sends:
        copy.wait_send()
    for copy in sends:
        copy.wait_send()


def shards(returns, weights):
    n_tm, n_paths = lax.axis_size("tm"), lax.axis_size("paths")
    steps, n_local, assets = returns.shape
    rows, port = weights.shape
    chunks = n_local // LANES
    half = steps // 2
    held = port // n_tm
    f32 = jnp.float32
    return pl.pallas_call(
        lambda *refs: kernel(n_tm, n_paths, *refs),
        name="drawdown",
        out_shape=jax.ShapeDtypeStruct((held, n_local), f32),
        in_specs=[pl.BlockSpec(memory_space=pltpu.HBM)] * 2,
        out_specs=pl.BlockSpec(memory_space=pltpu.VMEM),
        scratch_shapes=[
            pltpu.VMEM((chunks, steps, LANES, assets), jnp.bfloat16),
            pltpu.VMEM((rows, port), jnp.bfloat16),
            pltpu.VMEM((assets, LANES), jnp.bfloat16),
            pltpu.VMEM((half * LANES, LANES), f32),
            pltpu.VMEM((chunks, n_tm, 2, SUB, LANES), f32),
            pltpu.VMEM((chunks, n_tm, 2, SUB, LANES), f32),
            pltpu.SemaphoreType.DMA((chunks,)),
            pltpu.SemaphoreType.DMA,
            pltpu.SemaphoreType.DMA((n_paths,)),
            pltpu.SemaphoreType.DMA((n_paths,)),
            pltpu.SemaphoreType.DMA((chunks, n_tm)),
            pltpu.SemaphoreType.DMA((chunks, n_tm)),
        ],
        compiler_params=pltpu.CompilerParams(
            collective_id=0, has_side_effects=True, vmem_limit_bytes=67043328
        ),
    )(returns, weights)


def solution(mesh):
    in_specs = (P("tm", "paths", None), P("paths", None))
    out_specs = P("tm", "paths")
    return jax.shard_map(shards, mesh=mesh, in_specs=in_specs, out_specs=out_specs, check_vma=False)
```

time: 123 us -> 29.4 us (0.24); the launches traced: 121 us -> 29.3 us
  blocking collectives: 28.9 us -> 0 us
  Pallas kernels: 0 us -> 28 us
  other arithmetic: 25.8 us -> 0 us
  local copies, waits for them, and re-layouts: 24.7 us -> 1.3 us
  waiting for transfers between devices: 20.9 us -> 0 us
  starting transfers between devices: 11.8 us -> 0 us
  matrix products: 8.31 us -> 0 us
    all_to_all x2 -> x0, blocking collectives: 28.9 us -> none  [the longest x1 17.2 us: from_everyone(): lax.all_to_all(jnp.broadcast_to(array[None], (size, *array.shape)), axis,...]
    pallas_call x0 -> x1, Pallas kernels: none -> 28 us  [shards(): pl.pallas_call(lambda *refs: kernel(n_tm, n_paths, *refs), name='drawdown...]
    all_to_all x2 -> x0, waiting for transfers between devices: 20.9 us -> none  [from_everyone(): lax.all_to_all(jnp.broadcast_to(array[None], (size, *array.shape)), axis,...]
    another operation x1 -> x0, other arithmetic: 20.9 us -> none  [shards(): peaks = jnp.maximum(lax.cummax(values, axis=0), 0.0)]
    unnamed x15 -> x1, local copies, waits for them, and re-layouts: 20.4 us -> 1.3 us
    all_to_all x2 -> x0, starting transfers between devices: 11.8 us -> none  [from_everyone(): lax.all_to_all(jnp.broadcast_to(array[None], (size, *array.shape)), axis,...]
    dot_general x2 -> x0, matrix products: 8.31 us -> none  [the longest x1 6.03 us: shards(): jnp.einsum('tpa,aq->tqp', returns, all_weights, preferred_element_type=jn...]
    broadcast_in_dim x5 -> x0, local copies, waits for them, and re-layouts: 3.95 us -> none  [from_everyone(): jnp.broadcast_to(array[None], (size, *array.shape))]
  transfers between devices with their start and end apart: 2 -> 0, of which waited for: 2 -> 0; matrix products, arithmetic and copies ran while one was open for 27% -> 0% of each run, Pallas kernels for 0% -> 0%
where the time goes in v1:
time: 29.4 us; the launch traced here: 29.3 us
  Pallas kernels  28 us (95%)
  local copies, waits for them, and re-layouts  1.3 us (4%)
    pallas_call x1, Pallas kernels, shards(): pl.pallas_call(lambda *refs: kernel(n_tm, n_paths, *refs), name='drawdown...  28 us
    unnamed x1, local copies, waits for them, and re-layouts  1.3 us

profile of v1, /device:TPU:1, one launch (start us, length us, event | category | flops | bytes accessed | tf_op | source)
XLA Modules:
  0.0 29.3 jit_solution(13551096033286003625)
XLA Ops:
  0.0 28.0 %drawdown.1 = f32[4,512]{1,0:T(4,128)} custom-call(bf16[32,512,256]{2,1,0:T(8,128)(2,1)} %refs_0_.1, bf16[16,64]{1,0:T(8,128)(2,1)} %refs_1_.1), custom_call_target="tpu_custom_call" | custom-call | tf_op jit(solution)/shard_map/drawdown/pallas_call | solution.py:136
  28.0 1.3 %copy.4 = f32[4,512]{1,0:T(4,128)} copy(f32[4,512]{1,0:T(4,128)} %drawdown.1) | data formatting | bytes 16384

commit v2 on v1

v2 whole, which is shorter than its diff:
```python
import jax
import jax.numpy as jnp
from jax import lax
from jax.experimental import pallas as pl
from jax.experimental.pallas import tpu as pltpu
from jax.sharding import PartitionSpec as P

MESH = pl.DeviceIdType.MESH
LANES = 128
SUB = 8
SIDE = 4
PAIR = 2
HOPS = sorted(
    ((dx, dy) for dx in range(SIDE) for dy in range(SIDE) if dx or dy),
    key=lambda hop: -sum(min(d, SIDE - d) for d in hop),
)


def drawdown_kernel(n_tm, n_paths, returns_ref, w_ref, out_ref,
                    x, w_all, w_both, y, outbox, inbox,
                    x_sem, w_in_sem, w_send_sem, w_recv_sem, row_sem, send_sem, recv_sem):
    tm = lax.axis_index("tm")
    paths = lax.axis_index("paths")
    steps, n_local, assets = returns_ref.shape
    rows, port = w_ref.shape
    chunks = n_local // LANES
    half = steps // 2
    held = port // n_tm

    def column(j):
        return j + (paths <= j).astype(jnp.int32)

    def plane(dx, dy):
        return lax.rem(tm // SIDE + dx, SIDE) * SIDE + lax.rem(tm + dy, SIDE)

    barrier = pltpu.get_barrier_semaphore()
    for j in range(n_paths - 1):
        pl.semaphore_signal(barrier, inc=1, device_id=(tm, column(j)), device_id_type=MESH)
    for d in range(1, SIDE):
        pl.semaphore_signal(barrier, inc=1, device_id=(plane(d, 0), paths), device_id_type=MESH)
        pl.semaphore_signal(barrier, inc=1, device_id=(plane(0, d), paths), device_id_type=MESH)
    own_rows = pl.ds(pl.multiple_of(paths * rows, rows), rows)
    w_load = pltpu.make_async_copy(w_ref, w_all.at[own_rows, :], w_in_sem)
    w_load.start()
    x_load = pltpu.make_async_copy(returns_ref, x, x_sem)
    x_load.start()
    w_load.wait()

    pl.semaphore_wait(barrier, n_paths - 1 + 2 * (SIDE - 1))

    w_sends = []
    for j in range(n_paths - 1):
        copy = pltpu.make_async_remote_copy(
            src_ref=w_all.at[own_rows, :], dst_ref=w_all.at[own_rows, :],
            send_sem=w_send_sem.at[j], recv_sem=w_recv_sem.at[paths],
            device_id=(tm, column(j)), device_id_type=MESH)
        copy.start()
        w_sends.append(copy)
    for d in range(1, SIDE):
        pl.semaphore_signal(row_sem, inc=1, device_id=(plane(d, 0), paths), device_id_type=MESH)
    x_load.wait()
    pl.semaphore_wait(row_sem, SIDE - 1)
    for j in range(n_paths - 1):
        peer = column(j)
        rows_in = pl.ds(pl.multiple_of(peer * rows, rows), rows)
        pltpu.make_async_remote_copy(
            src_ref=w_all.at[rows_in, :], dst_ref=w_all.at[rows_in, :],
            send_sem=w_send_sem.at[j], recv_sem=w_recv_sem.at[peer],
            device_id=(tm, peer), device_id_type=MESH).wait_recv()

    source = lax.broadcasted_iota(jnp.int32, (port, LANES), 0)
    lane = lax.broadcasted_iota(jnp.int32, (port, LANES), 1)
    spread = jnp.where(source == (lane // SUB) * held + lane % held, 1.0, 0.0).astype(jnp.bfloat16)
    wide = jnp.dot(w_all[...], spread, preferred_element_type=jnp.float32)
    first = (lax.broadcasted_iota(jnp.int32, (assets, LANES), 1) % SUB) < held
    zeros = jnp.zeros((assets, LANES), jnp.bfloat16)
    for h, part in enumerate((jnp.where(first, wide, 0.0), jnp.where(first, 0.0, wide))):
        part = part.astype(jnp.bfloat16)
        for b in range(PAIR):
            rows_b = pl.ds((b * 2 + h) * assets, assets)
            for other in range(PAIR):
                w_both[rows_b, pl.ds(other * LANES, LANES)] = part if other == b else zeros

    second = (lax.broadcasted_iota(jnp.int32, (LANES, LANES), 1) % SUB) >= held
    group = 32
    sends = []
    for g in range(chunks // PAIR):
        for r in range(LANES // group):
            parts = [
                x[h * half:(h + 1) * half, pl.ds((g * PAIR + b) * LANES + r * group, group), :].reshape(half * group, assets)
                for b in range(PAIR) for h in range(2)
            ]
            y[g, r] = jnp.dot(jnp.concatenate(parts, axis=1), w_both[...], preferred_element_type=jnp.float32)
        for b in range(PAIR):
            c = g * PAIR + b
            lanes = pl.ds(b * LANES, LANES)
            total, high, low, deep = [], [], [], []
            for r in range(LANES // group):
                v = y[g, r, pl.ds(0, group), lanes]
                hi = jnp.maximum(v, 0.0)
                lo = jnp.minimum(v, 0.0)
                dd = hi - v
                for t in range(1, half):
                    v = v + y[g, r, pl.ds(t * group, group), lanes]
                    hi = jnp.maximum(hi, v)
                    lo = jnp.minimum(lo, v)
                    dd = jnp.maximum(dd, hi - v)
                total.append(v)
                high.append(hi)
                low.append(lo)
                deep.append(dd)
            total, high, low, deep = (jnp.concatenate(part, axis=0) for part in (total, high, low, deep))
            t0, h0, l0, d0 = (pltpu.roll(part, held, 1) for part in (total, high, low, deep))
            m_total = t0 + total
            m_high = jnp.maximum(h0, t0 + high)
            m_low = jnp.minimum(l0, t0 + low)
            m_deep = jnp.maximum(jnp.maximum(d0, deep), h0 - (t0 + low))
            th = jnp.where(second, m_high, pltpu.roll(m_total, LANES - held, 1))
            ld = jnp.where(second, m_deep, pltpu.roll(m_low, LANES - held, 1))
            outbox[c, :, 0] = th.T.reshape(n_tm, SUB, LANES)
            outbox[c, :, 1] = ld.T.reshape(n_tm, SUB, LANES)
            for j, hop in enumerate(HOPS):
                to = plane(*hop)
                copy = pltpu.make_async_remote_copy(
                    src_ref=outbox.at[c, to], dst_ref=inbox.at[c, tm],
                    send_sem=send_sem.at[c, j], recv_sem=recv_sem.at[c, tm],
                    device_id=(to, paths), device_id_type=MESH)
                copy.start()
                sends.append(copy)
            inbox[c, pl.ds(tm, 1)] = outbox[c, pl.ds(tm, 1)]

    for c in range(chunks):
        for j, hop in enumerate(HOPS):
            peer = plane(*hop)
            pltpu.make_async_remote_copy(
                src_ref=outbox.at[c, peer], dst_ref=inbox.at[c, peer],
                send_sem=send_sem.at[c, j], recv_sem=recv_sem.at[c, peer],
                device_id=(peer, paths), device_id_type=MESH).wait_recv()
        offset = jnp.zeros((SUB, LANES), jnp.float32)
        peak = jnp.zeros((SUB, LANES), jnp.float32)
        fall = jnp.zeros((SUB, LANES), jnp.float32)
        for s in range(n_tm):
            th = inbox[c, s, 0]
            ld = inbox[c, s, 1]
            fall = jnp.maximum(fall, jnp.maximum(pltpu.roll(ld, held, 0), peak - (offset + ld)))
            peak = jnp.maximum(peak, offset + pltpu.roll(th, held, 0))
            offset = offset + th
        out_ref[:, pl.ds(c * LANES, LANES)] = fall[:held]

    for copy in w_sends + sends:
        copy.wait_send()


def store_kernel(in_ref, out_ref, sem):
    copy = pltpu.make_async_copy(in_ref, out_ref, sem)
    copy.start()
    copy.wait()


def shards(returns, weights):
    n_tm, n_paths = lax.axis_size("tm"), lax.axis_size("paths")
    steps, n_local, assets = returns.shape
    rows, port = weights.shape
    chunks = n_local // LANES
    half = steps // 2
    held = port // n_tm
    f32, bf16 = jnp.float32, jnp.bfloat16
    vmem = pl.BlockSpec(memory_space=pltpu.VMEM)
    falls = pl.pallas_call(
        lambda *refs: drawdown_kernel(n_tm, n_paths, *refs),
        name="drawdown",
        out_shape=jax.ShapeDtypeStruct((held, n_local), f32),
        in_specs=[pl.BlockSpec(memory_space=pl.ANY)] * 2,
        out_specs=vmem,
        scratch_shapes=[
            pltpu.VMEM(returns.shape, bf16),
            pltpu.VMEM((assets, port), bf16),
            pltpu.VMEM((2 * PAIR * assets, PAIR * LANES), bf16),
            pltpu.VMEM((chunks // PAIR, LANES // 32, half * 32, PAIR * LANES), f32),
            pltpu.VMEM((chunks, n_tm, 2, SUB, LANES), f32),
            pltpu.VMEM((chunks, n_tm, 2, SUB, LANES), f32),
            pltpu.SemaphoreType.DMA,
            pltpu.SemaphoreType.DMA,
            pltpu.SemaphoreType.DMA((n_paths,)),
            pltpu.SemaphoreType.DMA((n_paths,)),
            pltpu.SemaphoreType.REGULAR,
            pltpu.SemaphoreType.DMA((chunks, n_tm)),
            pltpu.SemaphoreType.DMA((chunks, n_tm)),
        ],
        compiler_params=pltpu.CompilerParams(
            collective_id=0, has_side_effects=True, vmem_limit_bytes=44 * 1024 * 1024
        ),
    )(*(pltpu.with_memory_space_constraint(part, pltpu.HBM) for part in (returns, weights)))
    return pl.pallas_call(
        store_kernel,
        name="store",
        out_shape=jax.ShapeDtypeStruct((held, n_local), f32),
        in_specs=[vmem],
        out_specs=pl.BlockSpec(memory_space=pltpu.HBM),
        scratch_shapes=[pltpu.SemaphoreType.DMA],
        compiler_params=pltpu.CompilerParams(has_side_effects=True, vmem_limit_bytes=1024 * 1024),
    )(falls)


def solution(mesh):
    in_specs = (P("tm", "paths", None), P("paths", None))
    out_specs = P("tm", "paths")
    return jax.shard_map(shards, mesh=mesh, in_specs=in_specs, out_specs=out_specs, check_vma=False)
```

time: 29.4 us -> 26.5 us (0.901)
  Pallas kernels: 28 us -> 26.4 us
  local copies, waits for them, and re-layouts: 1.3 us -> 0 us
    pallas_call x1 -> x2, Pallas kernels: 28 us -> 26.4 us  [the longest x1 25.8 us: shards(): pl.pallas_call(lambda *refs: drawdown_kernel(n_tm, n_paths, *refs), name=...]
    unnamed x1 -> x0, local copies, waits for them, and re-layouts: 1.3 us -> none
where the time goes in v2:
time: 26.5 us; the launch traced here: 26.4 us
  Pallas kernels  26.4 us (100%)
    pallas_call x1, Pallas kernels, shards(): pl.pallas_call(lambda *refs: drawdown_kernel(n_tm, n_paths, *refs), name=...  25.8 us
    pallas_call x1, Pallas kernels, shards(): pl.pallas_call(store_kernel, name='store', out_shape=jax.ShapeDtypeStruct...  0.61 us

profile of v2, /device:TPU:1, one launch (start us, length us, event | category | flops | bytes accessed | tf_op | source)
XLA Modules:
  0.0 26.4 jit_solution(17806299378661798986)
XLA Ops:
  0.0 25.8 %drawdown.1.in_ref = f32[4,512]{1,0:T(4,128)S(1)} custom-call(bf16[32,512,256]{2,1,0:T(8,128)(2,1)} %refs_0_.1, bf16[16,64]{1,0:T(8,128)(2,1)} %refs_1_.1), custom_call_target="tpu_custom_call" | custom-call | tf_op jit(solution)/shard_map/drawdown/pallas_call | solution.py:169
  25.8 0.6 %store.1 = f32[4,512]{1,0:T(4,128)} custom-call(f32[4,512]{1,0:T(4,128)S(1)} %drawdown.1.in_ref), custom_call_target="tpu_custom_call" | custom-call | tf_op jit(solution)/shard_map/store/pallas_call | solution.py:194

commit v3 on v2

--- a/solution.py
+++ b/solution.py
@@ -10,6 +10,7 @@
 SUB = 8
 SIDE = 4
 PAIR = 2
+AHEAD = 2
 HOPS = sorted(
     ((dx, dy) for dx in range(SIDE) for dy in range(SIDE) if dx or dy),
     key=lambda hop: -sum(min(d, SIDE - d) for d in hop),
@@ -17,7 +18,7 @@
 
 
 def drawdown_kernel(n_tm, n_paths, returns_ref, w_ref, out_ref,
-                    x, w_all, w_both, y, outbox, inbox,
+                    x, w_in, w_all, w_both, y, outbox, inbox,
                     x_sem, w_in_sem, w_send_sem, w_recv_sem, row_sem, send_sem, recv_sem):
     tm = lax.axis_index("tm")
     paths = lax.axis_index("paths")
@@ -39,13 +40,30 @@
     for d in range(1, SIDE):
         pl.semaphore_signal(barrier, inc=1, device_id=(plane(d, 0), paths), device_id_type=MESH)
         pl.semaphore_signal(barrier, inc=1, device_id=(plane(0, d), paths), device_id_type=MESH)
-    own_rows = pl.ds(pl.multiple_of(paths * rows, rows), rows)
-    w_load = pltpu.make_async_copy(w_ref, w_all.at[own_rows, :], w_in_sem)
+    w_load = pltpu.make_async_copy(w_ref, w_in, w_in_sem)
     w_load.start()
     x_load = pltpu.make_async_copy(returns_ref, x, x_sem)
     x_load.start()
+
+    source = lax.broadcasted_iota(jnp.int32, (port, LANES), 0)
+    lane = lax.broadcasted_iota(jnp.int32, (port, LANES), 1)
+    spread = jnp.where(source == (lane // SUB) * held + lane % held, 1.0, 0.0).astype(jnp.bfloat16)
+    own_rows = pl.ds(pl.multiple_of(paths * rows, rows), rows)
     w_load.wait()
-
+    w_all[own_rows, :] = jnp.dot(w_in[...], spread, preferred_element_type=jnp.float32).astype(jnp.bfloat16)
+
+    first = (lax.broadcasted_iota(jnp.int32, (rows, LANES), 1) % SUB) < held
+    w_both[...] = jnp.zeros_like(w_both)
+
+    def lay_out(source):
+        wide = w_all[pl.ds(pl.multiple_of(source * rows, rows), rows), :].astype(jnp.float32)
+        for h, part in enumerate((jnp.where(first, wide, 0.0), jnp.where(first, 0.0, wide))):
+            part = part.astype(jnp.bfloat16)
+            for b in range(PAIR):
+                at = pl.multiple_of((b * 2 + h) * assets + source * rows, rows)
+                w_both[pl.ds(at, rows), pl.ds(b * LANES, LANES)] = part
+
+    lay_out(paths)
     pl.semaphore_wait(barrier, n_paths - 1 + 2 * (SIDE - 1))
 
     w_sends = []
@@ -67,32 +85,27 @@
             src_ref=w_all.at[rows_in, :], dst_ref=w_all.at[rows_in, :],
             send_sem=w_send_sem.at[j], recv_sem=w_recv_sem.at[peer],
             device_id=(tm, peer), device_id_type=MESH).wait_recv()
-
-    source = lax.broadcasted_iota(jnp.int32, (port, LANES), 0)
-    lane = lax.broadcasted_iota(jnp.int32, (port, LANES), 1)
-    spread = jnp.where(source == (lane // SUB) * held + lane % held, 1.0, 0.0).astype(jnp.bfloat16)
-    wide = jnp.dot(w_all[...], spread, preferred_element_type=jnp.float32)
-    first = (lax.broadcasted_iota(jnp.int32, (assets, LANES), 1) % SUB) < held
-    zeros = jnp.zeros((assets, LANES), jnp.bfloat16)
-    for h, part in enumerate((jnp.where(first, wide, 0.0), jnp.where(first, 0.0, wide))):
-        part = part.astype(jnp.bfloat16)
-        for b in range(PAIR):
-            rows_b = pl.ds((b * 2 + h) * assets, assets)
-            for other in range(PAIR):
-                w_both[rows_b, pl.ds(other * LANES, LANES)] = part if other == b else zeros
+        lay_out(peer)
 
     second = (lax.broadcasted_iota(jnp.int32, (LANES, LANES), 1) % SUB) >= held
     group = 32
     sends = []
-    for g in range(chunks // PAIR):
-        for r in range(LANES // group):
+    targets = [plane(*hop) for hop in HOPS]
+    targets = [jnp.where(tm == 0, targets[0], 0)] + [jnp.where(to == 0, targets[0], to) for to in targets[1:]]
+    def multiply(g, which):
+        for r in which:
             parts = [
                 x[h * half:(h + 1) * half, pl.ds((g * PAIR + b) * LANES + r * group, group), :].reshape(half * group, assets)
                 for b in range(PAIR) for h in range(2)
             ]
             y[g, r] = jnp.dot(jnp.concatenate(parts, axis=1), w_both[...], preferred_element_type=jnp.float32)
+
+    groups = LANES // group
+    multiply(0, range(groups))
+    for g in range(chunks // PAIR):
+        if g + 1 < chunks // PAIR:
+            multiply(g + 1, range(AHEAD))
         for b in range(PAIR):
-            c = g * PAIR + b
             lanes = pl.ds(b * LANES, LANES)
             total, high, low, deep = [], [], [], []
             for r in range(LANES // group):
@@ -117,35 +130,35 @@
             m_deep = jnp.maximum(jnp.maximum(d0, deep), h0 - (t0 + low))
             th = jnp.where(second, m_high, pltpu.roll(m_total, LANES - held, 1))
             ld = jnp.where(second, m_deep, pltpu.roll(m_low, LANES - held, 1))
-            outbox[c, :, 0] = th.T.reshape(n_tm, SUB, LANES)
-            outbox[c, :, 1] = ld.T.reshape(n_tm, SUB, LANES)
-            for j, hop in enumerate(HOPS):
-                to = plane(*hop)
-                copy = pltpu.make_async_remote_copy(
-                    src_ref=outbox.at[c, to], dst_ref=inbox.at[c, tm],
-                    send_sem=send_sem.at[c, j], recv_sem=recv_sem.at[c, tm],
-                    device_id=(to, paths), device_id_type=MESH)
-                copy.start()
-                sends.append(copy)
-            inbox[c, pl.ds(tm, 1)] = outbox[c, pl.ds(tm, 1)]
-
-    for c in range(chunks):
-        for j, hop in enumerate(HOPS):
+            outbox[g, :, b, 0] = th.T.reshape(n_tm, SUB, LANES)
+            outbox[g, :, b, 1] = ld.T.reshape(n_tm, SUB, LANES)
+        for to in targets:
+            copy = pltpu.make_async_remote_copy(
+                src_ref=outbox.at[g, to], dst_ref=inbox.at[g, tm],
+                send_sem=send_sem.at[g, to], recv_sem=recv_sem.at[g, tm],
+                device_id=(to, paths), device_id_type=MESH)
+            copy.start()
+            sends.append(copy)
+        inbox[g, pl.ds(tm, 1)] = outbox[g, pl.ds(tm, 1)]
+        if g + 1 < chunks // PAIR:
+            multiply(g + 1, range(AHEAD, groups))
+
+    for g in range(chunks // PAIR):
+        for hop in HOPS:
             peer = plane(*hop)
             pltpu.make_async_remote_copy(
-                src_ref=outbox.at[c, peer], dst_ref=inbox.at[c, peer],
-                send_sem=send_sem.at[c, j], recv_sem=recv_sem.at[c, peer],
+                src_ref=outbox.at[g, peer], dst_ref=inbox.at[g, peer],
+                send_sem=send_sem.at[g, peer], recv_sem=recv_sem.at[g, peer],
                 device_id=(peer, paths), device_id_type=MESH).wait_recv()
-        offset = jnp.zeros((SUB, LANES), jnp.float32)
-        peak = jnp.zeros((SUB, LANES), jnp.float32)
-        fall = jnp.zeros((SUB, LANES), jnp.float32)
+        offset = peak = fall = jnp.zeros((PAIR, SUB, LANES), jnp.float32)
         for s in range(n_tm):
-            th = inbox[c, s, 0]
-            ld = inbox[c, s, 1]
-            fall = jnp.maximum(fall, jnp.maximum(pltpu.roll(ld, held, 0), peak - (offset + ld)))
-            peak = jnp.maximum(peak, offset + pltpu.roll(th, held, 0))
+            th = inbox[g, s, :, 0]
+            ld = inbox[g, s, :, 1]
+            fall = jnp.maximum(fall, jnp.maximum(pltpu.roll(ld, held, 1), peak - (offset + ld)))
+            peak = jnp.maximum(peak, offset + pltpu.roll(th, held, 1))
             offset = offset + th
-        out_ref[:, pl.ds(c * LANES, LANES)] = fall[:held]
+        for b in range(PAIR):
+            out_ref[:, pl.ds((g * PAIR + b) * LANES, LANES)] = fall[b, :held]
 
     for copy in w_sends + sends:
         copy.wait_send()
@@ -174,18 +187,19 @@
         out_specs=vmem,
         scratch_shapes=[
             pltpu.VMEM(returns.shape, bf16),
-            pltpu.VMEM((assets, port), bf16),
+            pltpu.VMEM((rows, port), bf16),
+            pltpu.VMEM((assets, LANES), bf16),
             pltpu.VMEM((2 * PAIR * assets, PAIR * LANES), bf16),
             pltpu.VMEM((chunks // PAIR, LANES // 32, half * 32, PAIR * LANES), f32),
-            pltpu.VMEM((chunks, n_tm, 2, SUB, LANES), f32),
-            pltpu.VMEM((chunks, n_tm, 2, SUB, LANES), f32),
+            pltpu.VMEM((chunks // PAIR, n_tm, PAIR, 2, SUB, LANES), f32),
+            pltpu.VMEM((chunks // PAIR, n_tm, PAIR, 2, SUB, LANES), f32),
             pltpu.SemaphoreType.DMA,
             pltpu.SemaphoreType.DMA,
             pltpu.SemaphoreType.DMA((n_paths,)),
             pltpu.SemaphoreType.DMA((n_paths,)),
             pltpu.SemaphoreType.REGULAR,
-            pltpu.SemaphoreType.DMA((chunks, n_tm)),
-            pltpu.SemaphoreType.DMA((chunks, n_tm)),
+            pltpu.SemaphoreType.DMA((chunks // PAIR, n_tm)),
+            pltpu.SemaphoreType.DMA((chunks // PAIR, n_tm)),
         ],
         compiler_params=pltpu.CompilerParams(
             collective_id=0, has_side_effects=True, vmem_limit_bytes=44 * 1024 * 1024

time: 26.5 us -> 25.1 us (0.947)
  Pallas kernels: 26.4 us -> 25 us
    pallas_call x1, Pallas kernels: 25.8 us -> 24.4 us  [shards(): pl.pallas_call(lambda *refs: drawdown_kernel(n_tm, n_paths, *refs), name=...]
where the time goes in v3:
time: 25.1 us; the launch traced here: 25 us
  Pallas kernels  25 us (100%)
    pallas_call x1, Pallas kernels, shards(): pl.pallas_call(lambda *refs: drawdown_kernel(n_tm, n_paths, *refs), name=...  24.4 us
    pallas_call x1, Pallas kernels, shards(): pl.pallas_call(store_kernel, name='store', out_shape=jax.ShapeDtypeStruct...  0.61 us

profile of v3, /device:TPU:1, one launch (start us, length us, event | category | flops | bytes accessed | tf_op | source)
XLA Modules:
  0.0 25.0 jit_solution(5176433198549910570)
XLA Ops:
  0.0 24.4 %drawdown.1.in_ref = f32[4,512]{1,0:T(4,128)S(1)} custom-call(bf16[32,512,256]{2,1,0:T(8,128)(2,1)} %refs_0_.1, bf16[16,64]{1,0:T(8,128)(2,1)} %refs_1_.1), custom_call_target="tpu_custom_call" | custom-call | tf_op jit(solution)/shard_map/drawdown/pallas_call | solution.py:182
  24.4 0.6 %store.1 = f32[4,512]{1,0:T(4,128)} custom-call(f32[4,512]{1,0:T(4,128)S(1)} %drawdown.1.in_ref), custom_call_target="tpu_custom_call" | custom-call | tf_op jit(solution)/shard_map/store/pallas_call | solution.py:208

commit v4 on v3

--- a/solution.py
+++ b/solution.py
@@ -19,7 +19,7 @@
 
 def drawdown_kernel(n_tm, n_paths, returns_ref, w_ref, out_ref,
                     x, w_in, w_all, w_both, y, outbox, inbox,
-                    x_sem, w_in_sem, w_send_sem, w_recv_sem, row_sem, send_sem, recv_sem):
+                    x_sem, w_in_sem, w_send_sem, w_recv_sem, late_sem, row_sem, send_sem, recv_sem):
     tm = lax.axis_index("tm")
     paths = lax.axis_index("paths")
     steps, n_local, assets = returns_ref.shape
@@ -35,8 +35,13 @@
         return lax.rem(tm // SIDE + dx, SIDE) * SIDE + lax.rem(tm + dy, SIDE)
 
     barrier = pltpu.get_barrier_semaphore()
+    late = paths >= n_paths // 2
     for j in range(n_paths - 1):
-        pl.semaphore_signal(barrier, inc=1, device_id=(tm, column(j)), device_id_type=MESH)
+        to = column(j)
+
+        @pl.when(jnp.logical_not(jnp.logical_and(late, to < n_paths // 2)))
+        def _(to=to):
+            pl.semaphore_signal(barrier, inc=1, device_id=(tm, to), device_id_type=MESH)
     for d in range(1, SIDE):
         pl.semaphore_signal(barrier, inc=1, device_id=(plane(d, 0), paths), device_id_type=MESH)
         pl.semaphore_signal(barrier, inc=1, device_id=(plane(0, d), paths), device_id_type=MESH)
@@ -52,59 +57,84 @@
     w_load.wait()
     w_all[own_rows, :] = jnp.dot(w_in[...], spread, preferred_element_type=jnp.float32).astype(jnp.bfloat16)
 
+    team = n_paths // 2
+    mine = paths // team
+    depth = team * rows
     first = (lax.broadcasted_iota(jnp.int32, (rows, LANES), 1) % SUB) < held
     w_both[...] = jnp.zeros_like(w_both)
 
-    def lay_out(source):
+    def lay_out(source, stage):
         wide = w_all[pl.ds(pl.multiple_of(source * rows, rows), rows), :].astype(jnp.float32)
         for h, part in enumerate((jnp.where(first, wide, 0.0), jnp.where(first, 0.0, wide))):
             part = part.astype(jnp.bfloat16)
             for b in range(PAIR):
-                at = pl.multiple_of((b * 2 + h) * assets + source * rows, rows)
-                w_both[pl.ds(at, rows), pl.ds(b * LANES, LANES)] = part
-
-    lay_out(paths)
-    pl.semaphore_wait(barrier, n_paths - 1 + 2 * (SIDE - 1))
-
-    w_sends = []
-    for j in range(n_paths - 1):
-        copy = pltpu.make_async_remote_copy(
-            src_ref=w_all.at[own_rows, :], dst_ref=w_all.at[own_rows, :],
-            send_sem=w_send_sem.at[j], recv_sem=w_recv_sem.at[paths],
-            device_id=(tm, column(j)), device_id_type=MESH)
+                at = pl.multiple_of((b * 2 + h) * depth + lax.rem(source, team) * rows, rows)
+                w_both[stage, pl.ds(at, rows), pl.ds(b * LANES, LANES)] = part
+
+    lay_out(paths, 0)
+    pl.semaphore_wait(barrier, n_paths // 2 - 1 + 2 * (SIDE - 1) + late.astype(jnp.int32) * (n_paths // 2))
+
+    own_team = [mine * team + j + (lax.rem(paths, team) <= j).astype(jnp.int32) for j in range(team - 1)]
+    other_team = [(1 - mine) * team + j for j in range(team)]
+
+    def carry(source, to):
+        at = pl.ds(pl.multiple_of(source * rows, rows), rows)
+        return pltpu.make_async_remote_copy(
+            src_ref=w_all.at[at, :], dst_ref=w_all.at[at, :],
+            send_sem=w_send_sem.at[to], recv_sem=w_recv_sem.at[source],
+            device_id=(tm, to), device_id_type=MESH)
+
+    to_own = [carry(paths, to) for to in own_team]
+    to_other = [carry(paths, to) for to in other_team]
+    @pl.when(late)
+    def _():
+        for to in other_team:
+            pl.semaphore_signal(late_sem, inc=1, device_id=(tm, to), device_id_type=MESH)
+        for copy in to_other:
+            copy.start()
+
+    for copy in to_own:
         copy.start()
-        w_sends.append(copy)
+    w_sends = to_own + to_other
     for d in range(1, SIDE):
         pl.semaphore_signal(row_sem, inc=1, device_id=(plane(d, 0), paths), device_id_type=MESH)
-    x_load.wait()
-    pl.semaphore_wait(row_sem, SIDE - 1)
-    for j in range(n_paths - 1):
-        peer = column(j)
-        rows_in = pl.ds(pl.multiple_of(peer * rows, rows), rows)
-        pltpu.make_async_remote_copy(
-            src_ref=w_all.at[rows_in, :], dst_ref=w_all.at[rows_in, :],
-            send_sem=w_send_sem.at[j], recv_sem=w_recv_sem.at[peer],
-            device_id=(tm, peer), device_id_type=MESH).wait_recv()
-        lay_out(peer)
-
     second = (lax.broadcasted_iota(jnp.int32, (LANES, LANES), 1) % SUB) >= held
     group = 32
     sends = []
     targets = [plane(*hop) for hop in HOPS]
     targets = [jnp.where(tm == 0, targets[0], 0)] + [jnp.where(to == 0, targets[0], to) for to in targets[1:]]
-    def multiply(g, which):
+    def multiply(stage, g, which):
+        side = mine if stage == 0 else 1 - mine
+        columns = pl.ds(pl.multiple_of(side * depth, depth), depth)
         for r in which:
             parts = [
-                x[h * half:(h + 1) * half, pl.ds((g * PAIR + b) * LANES + r * group, group), :].reshape(half * group, assets)
+                x[h * half:(h + 1) * half, pl.ds((g * PAIR + b) * LANES + r * group, group), columns].reshape(half * group, depth)
                 for b in range(PAIR) for h in range(2)
             ]
-            y[g, r] = jnp.dot(jnp.concatenate(parts, axis=1), w_both[...], preferred_element_type=jnp.float32)
+            share = jnp.dot(jnp.concatenate(parts, axis=1), w_both[stage], preferred_element_type=jnp.float32)
+            y[g, r] = share if stage == 0 else y[g, r] + share
 
     groups = LANES // group
-    multiply(0, range(groups))
+    for peer in own_team:
+        carry(peer, peer).wait_recv()
+        lay_out(peer, 0)
+    x_load.wait()
+    for g in range(chunks // PAIR):
+        multiply(0, g, range(groups))
+
+    @pl.when(jnp.logical_not(late))
+    def _():
+        pl.semaphore_wait(late_sem, team)
+        for copy in to_other:
+            copy.start()
+
+    for peer in other_team:
+        carry(peer, peer).wait_recv()
+        lay_out(peer, 1)
+    multiply(1, 0, range(groups))
     for g in range(chunks // PAIR):
         if g + 1 < chunks // PAIR:
-            multiply(g + 1, range(AHEAD))
+            multiply(1, g + 1, range(AHEAD))
         for b in range(PAIR):
             lanes = pl.ds(b * LANES, LANES)
             total, high, low, deep = [], [], [], []
@@ -132,6 +162,8 @@
             ld = jnp.where(second, m_deep, pltpu.roll(m_low, LANES - held, 1))
             outbox[g, :, b, 0] = th.T.reshape(n_tm, SUB, LANES)
             outbox[g, :, b, 1] = ld.T.reshape(n_tm, SUB, LANES)
+        if g == 0:
+            pl.semaphore_wait(row_sem, SIDE - 1)
         for to in targets:
             copy = pltpu.make_async_remote_copy(
                 src_ref=outbox.at[g, to], dst_ref=inbox.at[g, tm],
@@ -141,7 +173,7 @@
             sends.append(copy)
         inbox[g, pl.ds(tm, 1)] = outbox[g, pl.ds(tm, 1)]
         if g + 1 < chunks // PAIR:
-            multiply(g + 1, range(AHEAD, groups))
+            multiply(1, g + 1, range(AHEAD, groups))
 
     for g in range(chunks // PAIR):
         for hop in HOPS:
@@ -189,7 +221,7 @@
             pltpu.VMEM(returns.shape, bf16),
             pltpu.VMEM((rows, port), bf16),
             pltpu.VMEM((assets, LANES), bf16),
-            pltpu.VMEM((2 * PAIR * assets, PAIR * LANES), bf16),
+            pltpu.VMEM((2, PAIR * assets, PAIR * LANES), bf16),
             pltpu.VMEM((chunks // PAIR, LANES // 32, half * 32, PAIR * LANES), f32),
             pltpu.VMEM((chunks // PAIR, n_tm, PAIR, 2, SUB, LANES), f32),
             pltpu.VMEM((chunks // PAIR, n_tm, PAIR, 2, SUB, LANES), f32),
@@ -197,6 +229,7 @@
             pltpu.SemaphoreType.DMA,
             pltpu.SemaphoreType.DMA((n_paths,)),
             pltpu.SemaphoreType.DMA((n_paths,)),
+            pltpu.SemaphoreType.REGULAR,
             pltpu.SemaphoreType.REGULAR,
             pltpu.SemaphoreType.DMA((chunks // PAIR, n_tm)),
             pltpu.SemaphoreType.DMA((chunks // PAIR, n_tm)),

time: 25.1 us -> 24.8 us (0.988)
  Pallas kernels: 25 us -> 24.7 us
    pallas_call x1, Pallas kernels: 24.4 us -> 24.1 us  [shards(): pl.pallas_call(lambda *refs: drawdown_kernel(n_tm, n_paths, *refs), name=...]
where the time goes in v4:
time: 24.8 us; the launch traced here: 24.7 us
  Pallas kernels  24.7 us (100%)
    pallas_call x1, Pallas kernels, shards(): pl.pallas_call(lambda *refs: drawdown_kernel(n_tm, n_paths, *refs), name=...  24.1 us
    pallas_call x1, Pallas kernels, shards(): pl.pallas_call(store_kernel, name='store', out_shape=jax.ShapeDtypeStruct...  0.61 us

profile of v4, /device:TPU:1, one launch (start us, length us, event | category | flops | bytes accessed | tf_op | source)
XLA Modules:
  0.0 24.7 jit_solution(9490824016986263578)
XLA Ops:
  0.0 24.1 %drawdown.1.in_ref = f32[4,512]{1,0:T(4,128)S(1)} custom-call(bf16[32,512,256]{2,1,0:T(8,128)(2,1)} %refs_0_.1, bf16[16,64]{1,0:T(8,128)(2,1)} %refs_1_.1), custom_call_target="tpu_custom_call" | custom-call | tf_op jit(solution)/shard_map/drawdown/pallas_call | solution.py:214
  24.1 0.6 %store.1 = f32[4,512]{1,0:T(4,128)} custom-call(f32[4,512]{1,0:T(4,128)S(1)} %drawdown.1.in_ref), custom_call_target="tpu_custom_call" | custom-call | tf_op jit(solution)/shard_map/store/pallas_call | solution.py:241
